TPU v7x, 256 devices: a whole 4x4x8 slice. The times are simulated.
256 devices in a mesh: dp: 32 (over x, z_lo, core), head: 8 (over y, z_hi).
Axes of the slice: x: 4, y: 4, z: 8 (z_hi: 2, z_lo: 4; z = z_hi * 4 + z_lo), core: 2. Of those that a mesh axis runs over, the one named last changes fastest.
Arguments:
- frames_in: bfloat16 [32, 8, 320, 640], P('dp', 'head'), may hold values from -6 to 6
- ln1_gain: float32 [1280], replicated, may hold values from 0.25 to 1.75
- ln1_bias: float32 [1280], replicated, may hold values from -3 to 3
- qkv_weight: bfloat16 [1280, 3, 1024], P('dp', None, 'head'), may hold values from -0.1875 to 0.1875
- qv_bias: float32 [2, 1024], P(None, 'head'), may hold values from -3 to 3
- out_weight: bfloat16 [1024, 1280], P(('head', 'dp')), may hold values from -0.1875 to 0.1875
- out_bias: float32 [1280], P('head'), may hold values from -3 to 3
- ln2_gain: float32 [1280], replicated, may hold values from 0.25 to 1.75
- ln2_bias: float32 [1280], replicated, may hold values from -3 to 3
- fc1_weight: bfloat16 [1280, 5120], P('dp', 'head'), may hold values from -0.15625 to 0.15625
- fc1_bias: float32 [5120], P('head'), may hold values from -3 to 3
- fc2_weight: bfloat16 [5120, 1280], P(('head', 'dp')), may hold values from -0.078125 to 0.078125
- fc2_bias: float32 [1280], P('head'), may hold values from -3 to 3
- server_of_clip: int32 [32], replicated, may hold values from 0 to 7
Outputs:
- encoded: bfloat16 [32, 8, 320, 640], P('dp', 'head')
All inputs are finite; a program needn't handle non-finite values.
Results may differ from a plain program's by a relative error of at most 0.014.
Values may be sent and summed in bfloat16 or wider, within the bound.
No kernel may reach another device: no remote copies, remote signals or barrier semaphores. Data moves between devices by JAX's collectives and lax.ppermute only.
A program may use at most 64 MiB of HBM per device.

v0:
```python
import jax
import jax.numpy as jnp
from jax import lax
from jax.sharding import Mesh
from jax.sharding import PartitionSpec as P

HDIM = 64
DP = ("x", "zl", "core")
HEAD = ("y", "zh")
EPS = 1e-05


def exchange(value, axes):
    return lax.all_to_all(value, axes, split_axis=0, concat_axis=0, tiled=True)


def gather_y(value):
    copies = jnp.broadcast_to(value[None], (4, *value.shape))
    return exchange(copies, "y").reshape(4 * value.shape[0], value.shape[1])


def norm_columns(matrix, gain, shift):
    floats = matrix.astype(jnp.float32)
    center = jnp.mean(floats, axis=0, keepdims=True)
    spread = jnp.mean(jnp.square(floats - center), axis=0, keepdims=True)
    return ((floats - center) * lax.rsqrt(spread + EPS) * gain[:, None] + shift[:, None]).astype(
        jnp.bfloat16
    )


def dot_rows(left, right):
    return lax.dot_general(
        left, right, (((0,), (0,)), ((), ())), preferred_element_type=jnp.float32
    )


def slot_order(server_list):
    clip_count = server_list.shape[0]
    indices = jnp.arange(clip_count, dtype=jnp.int32)
    earlier = (server_list[None, :] < server_list[:, None]) | (
        server_list[None, :] == server_list[:, None]
    ) & (indices[None, :] < indices[:, None])
    slot_of = jnp.sum(earlier.astype(jnp.int32), axis=1)
    return jnp.sum(jnp.where(slot_of[None, :] == indices[:, None], indices[None, :], 0), axis=1)


def attend(queries, key_rows, value_rows):
    outs = []
    for at in range(0, queries.shape[0], HDIM):
        scores = dot_rows(key_rows[at : at + HDIM], queries[at : at + HDIM])
        maxima = jnp.max(scores, axis=0, keepdims=True)
        weights = jnp.exp(scores - maxima)
        probs = (weights / jnp.sum(weights, axis=0, keepdims=True)).astype(jnp.bfloat16)
        outs.append(
            jnp.dot(value_rows[at : at + HDIM], probs, preferred_element_type=jnp.float32).astype(
                jnp.bfloat16
            )
        )
    return jnp.concatenate(outs, axis=0)


def on_device(
    frames_in,
    ln1_gain,
    ln1_bias,
    qkv_weight,
    qv_bias,
    out_weight,
    out_bias,
    ln2_gain,
    ln2_bias,
    fc1_weight,
    fc1_bias,
    fc2_weight,
    fc2_bias,
    server_of_clip,
):
    bf16 = jnp.bfloat16
    y_at, core_at, zh_at = (lax.axis_index("y"), lax.axis_index("core"), lax.axis_index("zh"))
    plane = ("zh", "x", "zl", "core")
    w_qkv = lax.all_gather(qkv_weight.reshape(40, 384), plane, axis=0, tiled=True)
    w_out = lax.all_gather(out_weight, ("y",) + plane, axis=0, tiled=True)
    w_one = lax.all_gather(fc1_weight, plane, axis=0, tiled=True)
    w_two = lax.all_gather(fc2_weight, plane, axis=0, tiled=True)
    own = jnp.concatenate([qv_bias[0], qv_bias[1], fc1_bias, fc2_bias, out_bias])
    other = lax.ppermute(own, "zh", [(0, 1), (1, 0)])
    both = jnp.where(zh_at == 0, jnp.stack([own, other]), jnp.stack([other, own]))
    q_bias = both[:, 0:128].reshape(256, 1)
    v_bias = both[:, 128:256].reshape(256, 1)
    one_bias = both[:, 256:896].reshape(1280, 1)
    two_bias = both[:, 896:1056].reshape(320, 1)
    out_pair = both[:, 1056:1216].reshape(320)
    out_all = jnp.zeros((4, 320), jnp.float32)
    out_all = lax.dynamic_update_slice(out_all, out_pair[None], (y_at, 0))
    for step in (1, 2, 3):
        part = lax.ppermute(out_pair, "y", [(at, (at + step) % 4) for at in range(4)])
        out_all = lax.dynamic_update_slice(out_all, part[None], ((y_at - step) % 4, 0))
    out_all = out_all.reshape(1280, 1)
    clip_order = slot_order(server_of_clip)
    source_at = clip_order % 2 * 16 + clip_order // 2
    source_at = source_at.reshape(16, 2).T.reshape(32)
    pieces = frames_in[0, 0].reshape(2, 160, 4, 160).transpose(0, 3, 2, 1).reshape(32, 10, 640)
    shuffled = exchange(pieces, ("core", "x", "zl"))
    picked = jnp.take(shuffled, source_at, axis=0)
    block = exchange(picked, ("zh", "x", "zl")).reshape(320, 640)
    residual = gather_y(block)
    normed_one = norm_columns(residual, ln1_gain, ln1_bias)
    halves = [dot_rows(w_qkv[at : at + 1280], normed_one) for at in (0, 1280)]
    queries = jnp.concatenate([half[0:128] for half in halves], axis=0)
    queries = ((queries + q_bias) * HDIM ** (-0.5)).astype(bf16)
    keys = jnp.concatenate([half[128:256] for half in halves], axis=0).astype(bf16)
    values = jnp.concatenate([half[256:384] for half in halves], axis=0)
    values = (values + v_bias).astype(bf16)
    mine = jnp.concatenate([keys, values], axis=0)
    theirs = lax.ppermute(mine, "core", [(0, 1), (1, 0)])
    every = jnp.concatenate([mine, theirs], axis=1)
    context = attend(queries, every[:256], every[256:])
    whole_context = gather_y(context)
    attended = (residual.astype(jnp.float32) + out_all + dot_rows(w_out, whole_context)).astype(
        bf16
    )
    normed_two = norm_columns(attended, ln2_gain, ln2_bias)
    sums = jnp.concatenate(
        [dot_rows(w_one[at : at + 1280], normed_two) for at in (0, 1280)], axis=0
    )
    hidden = jax.nn.gelu(sums + one_bias, approximate=False).astype(bf16)
    terms = dot_rows(w_two, hidden).astype(bf16).reshape(4, 320, 640)
    arrived = exchange(terms, "y").astype(jnp.float32)
    kept = lax.dynamic_slice(attended, (y_at * 320, 0), (320, 640)).astype(jnp.float32)
    done = (kept + two_bias + jnp.sum(arrived, axis=0)).astype(bf16).reshape(2, 160, 640)
    same = [(j * 2 + k, k * 2 + j) for k in range(2) for j in range(2)]
    cross = [(j * 2 + k, k * 2 + 1 - j) for k in range(2) for j in range(2)]
    first = lax.ppermute(jnp.where(core_at == 0, done[0], done[1]), ("core", "zh"), same)
    second = lax.ppermute(jnp.where(core_at == 0, done[1], done[0]), ("core", "zh"), cross)
    halves = jnp.where(zh_at == 0, jnp.stack([first, second]), jnp.stack([second, first]))
    return halves.reshape(2, 160, 4, 160).transpose(0, 3, 2, 1).reshape(1, 1, 320, 640)


def solution(mesh):
    torus = Mesh(mesh.devices.reshape(4, 4, 2, 4, 2), ("x", "zl", "core", "y", "zh"))
    return jax.shard_map(
        on_device,
        mesh=torus,
        in_specs=(
            P(DP, HEAD, None, None),
            P(),
            P(),
            P(DP, None, HEAD),
            P(None, HEAD),
            P(HEAD + DP, None),
            P(HEAD),
            P(),
            P(),
            P(DP, HEAD),
            P(HEAD),
            P(HEAD + DP, None),
            P(HEAD),
            P(),
        ),
        out_specs=P(DP, HEAD, None, None),
        check_vma=False,
    )
```

profile of v0, /device:TPU:3, one launch (start us, length us, event | category | flops | bytes accessed | tf_op | source)
XLA Modules:
  0.0 857.3 jit_solution(10657175189306649570)
XLA Ops:
  13.1 9.3 %all-to-all-start = ((bf16[32,10,640]{2,1,0:T(8,128)(2,1)}), bf16[32,10,640]{2,1,0:T(8,128)(2,1)S(1)}, u32[]{:S(2)}, u32[]{:S(2)}) async-start(bf16[32,10,640]{2,1,0:T(8,128)(2,1)} %reshape.133), calls=%async_computation | async-start | bytes 1310720 | tf_op jit(solution)/shard_map/all_to_all | solution.py:14
  23.1 17.5 %all-to-all-done = bf16[32,10,640]{2,1,0:T(8,128)(2,1)S(1)} async-done(((bf16[32,10,640]{2,1,0:T(8,128)(2,1)}), bf16[32,10,640]{2,1,0:T(8,128)(2,1)S(1)}, u32[]{:S(2)}, u32[]{:S(2)}) %all-to-all-start) | async-done | bytes 409632 | tf_op jit(solution)/shard_map/all_to_all | solution.py:14
  41.4 28.5 %all_to_all.25 = bf16[32,10,640]{2,1,0:T(8,128)(2,1)S(1)} all-to-all(bf16[32,10,640]{2,1,0:T(8,128)(2,1)S(1)} %broadcast_select_fusion), channel_id=1, replica_groups=mesh['x'=4,'zl'=4,'core'=2,'y'=4,'zh'=2] {'zh','x','zl'}, dimensions={0} | all-to-all | bytes 819200 | tf_op jit(solution)/shard_map/all_to_all | solution.py:14
  71.4 4.6 all-to-all-start.2
  77.6 5.0 collective-permute-done
  82.6 13.7 %all-to-all-done.2 = bf16[4,320,640]{2,1,0:T(8,128)(2,1)S(1)} async-done(((bf16[4,320,640]{2,1,0:T(8,128)(2,1)}), bf16[4,320,640]{2,1,0:T(8,128)(2,1)S(1)}, u32[]{:S(2)}, u32[]{:S(2)}) %all-to-all-start.2) | async-done | bytes 1638432 | tf_op jit(solution)/shard_map/all_to_all | solution.py:14
  97.8 30.2 %all-gather.7.cloned.1.call-done = bf16[2560,384]{1,0:T(8,128)(2,1)} async-done(((bf16[40,384]{1,0:T(8,128)(2,1)}), bf16[2560,384]{1,0:T(8,128)(2,1)}) %all-gather.7.cloned.1.call-update) | async-done | bytes 1966096 | tf_op jit(solution)/shard_map/all_gather | solution.py:81
  145.1 4.3 all-to-all-start.3
  154.7 9.1 %collective-permute-done.1 = f32[320]{0:T(512)S(1)} collective-permute-done((f32[320]{0:T(512)S(1)}, f32[320]{0:T(512)S(1)}, u32[]{:S(2)}, u32[]{:S(2)}) %collective-permute-start.1) | collective-permute-done | bytes 1312 | tf_op jit(solution)/shard_map/ppermute | solution.py:96
  163.8 3.4 collective-permute-done.2
  170.1 373.0 %all-gather.11.cloned.1.call-done = bf16[256,4,1280]{2,1,0:T(4,128)(2,1)} async-done(((bf16[1,4,1280]{2,1,0:T(4,128)(2,1)}), bf16[256,4,1280]{2,1,0:T(4,128)(2,1)}) %all-gather.11.cloned.1.call-update) | async-done | bytes 2621456 | tf_op jit(solution)/shard_map/all_gather | solution.py:82
  543.1 5.3 reshape.150
  548.5 4.2 convert_reduce_fusion
  554.5 107.6 %all-gather.9.cloned.1.call-done = bf16[2560,640]{1,0:T(8,128)(2,1)} async-done(((bf16[40,640]{1,0:T(8,128)(2,1)}), bf16[2560,640]{1,0:T(8,128)(2,1)}) %all-gather.9.cloned.1.call-update) | async-done | bytes 3276816 | tf_op jit(solution)/shard_map/all_gather | solution.py:83
  662.2 5.0 fusion.61
  670.1 108.1 %all-gather.13.cloned.1.call-done = bf16[64,20,1280]{2,1,0:T(8,128)(2,1)} async-done(((bf16[1,20,1280]{2,1,0:T(8,128)(2,1)}), bf16[64,20,1280]{2,1,0:T(8,128)(2,1)}) %all-gather.13.cloned.1.call-update) | async-done | bytes 3276816 | tf_op jit(solution)/shard_map/all_gather | solution.py:84
  778.2 4.9 reshape.152
  783.1 12.1 %fusion.20 = bf16[1280,640]{0,1:T(8,128)(2,1)} fusion(bf16[1280,1280]{1,0:T(8,128)(2,1)S(1)} %reshape.152, f32[640,640]{1,0:T(8,128)} %fusion.64, f32[640,640]{1,0:T(8,128)} %fusion.61, f32[1280]{0:T(1024)S(1)} %add.183), kind=kOutput, calls=%fused_computation.47 | convolution fusion | flops 2152857600 | bytes 8197120 | tf_op jit(solution)/shard_map/dot_general | solution.py:32
  795.2 3.5 copy.38
  798.7 4.0 all-to-all-start.4
  802.8 20.9 %all-to-all-done.4 = bf16[4,320,640]{2,1,0:T(8,128)(2,1)S(1)} async-done(((bf16[4,320,640]{2,1,0:T(8,128)(2,1)}), bf16[4,320,640]{2,1,0:T(8,128)(2,1)S(1)}, u32[]{:S(2)}, u32[]{:S(2)}) %all-to-all-start.4) | async-done | bytes 1638432 | tf_op jit(solution)/shard_map/all_to_all | solution.py:14
  825.7 6.3 collective-permute-start.5
  832.1 13.2 %collective-permute-done.5 = bf16[160,640]{0,1:T(8,128)(2,1)S(1)} collective-permute-done((bf16[160,640]{0,1:T(8,128)(2,1)S(1)}, bf16[160,640]{0,1:T(8,128)(2,1)S(1)}, u32[]{:S(2)}, u32[]{:S(2)}) %collective-permute-start.5) | collective-permute-done | bytes 204832 | tf_op jit(solution)/shard_map/ppermute | solution.py:133
  845.3 3.3 collective-permute-done.6
  (128 shorter events, 46.4 us)
Async XLA Ops:
  6.5 15.9 %copy-start.15 = (s32[32]{0:T(128)S(1)}, s32[32]{0:T(128)}, u32[]{:S(2)}) copy-start(s32[32]{0:T(128)} %param.27) | copy-start | bytes 388
  6.5 121.4 %all-gather.7.cloned.1.call-start = ((), (), s32[]{:S(2)}) async-start(), calls=%async_computation.5 | async-start | bytes 1996800 | tf_op jit(solution)/shard_map/all_gather | solution.py:81
  7.9 535.2 %all-gather.11.cloned.1.call-start = ((), (), s32[]{:S(2)}) async-start(), calls=%async_computation.7 | async-start | bytes 2631680 | tf_op jit(solution)/shard_map/all_gather | solution.py:82
  8.7 653.5 %all-gather.9.cloned.1.call-start = ((), (), s32[]{:S(2)}) async-start(), calls=%async_computation.6 | async-start | bytes 3328000 | tf_op jit(solution)/shard_map/all_gather | solution.py:83
  13.1 27.5 %all-to-all-start = ((bf16[32,10,640]{2,1,0:T(8,128)(2,1)}), bf16[32,10,640]{2,1,0:T(8,128)(2,1)S(1)}, u32[]{:S(2)}, u32[]{:S(2)}) async-start(bf16[32,10,640]{2,1,0:T(8,128)(2,1)} %reshape.133), calls=%async_computation | async-start | bytes 1310720 | tf_op jit(solution)/shard_map/all_to_all | solution.py:14
  69.9 6.1 copy-start.10
  71.4 25.7 %copy-start.5 = (f32[1280]{0:T(1024)S(1)}, f32[1280]{0:T(1024)}, u32[]{:S(2)}) copy-start(f32[1280]{0:T(1024)} %param.16) | copy-start | bytes 15364
  71.4 25.7 %copy-start.6 = (f32[1280]{0:T(1024)S(1)}, f32[1280]{0:T(1024)}, u32[]{:S(2)}) copy-start(f32[1280]{0:T(1024)} %param.15) | copy-start | bytes 15364
  71.4 24.9 %all-to-all-start.2 = ((bf16[4,320,640]{2,1,0:T(8,128)(2,1)}), bf16[4,320,640]{2,1,0:T(8,128)(2,1)S(1)}, u32[]{:S(2)}, u32[]{:S(2)}) async-start(bf16[4,320,640]{2,1,0:T(8,128)(2,1)} %broadcast_in_dim.38), calls=%async_computation.2 | async-start | bytes 3276800 | tf_op jit(solution)/shard_map/all_to_all | solution.py:14
  76.0 702.2 %all-gather.13.cloned.1.call-start = ((), (), s32[]{:S(2)}) async-start(), calls=%async_computation.8 | async-start | bytes 3993600 | tf_op jit(solution)/shard_map/all_gather | solution.py:84
  76.2 6.4 collective-permute-start
  132.4 2.9 collective-permute-start.4
  145.1 403.4 %all-to-all-start.3 = ((bf16[4,256,640]{2,1,0:T(8,128)(2,1)}), bf16[4,256,640]{2,1,0:T(8,128)(2,1)}, u32[]{:S(2)}, u32[]{:S(2)}) async-start(bf16[4,256,640]{2,1,0:T(8,128)(2,1)} %broadcast_in_dim.43), calls=%async_computation.3 | async-start | bytes 2621440 | tf_op jit(solution)/shard_map/all_to_all | solution.py:14
  149.6 14.2 %collective-permute-start.1 = (f32[320]{0:T(512)S(1)}, f32[320]{0:T(512)S(1)}, u32[]{:S(2)}, u32[]{:S(2)}) collective-permute-start(f32[320]{0:T(512)S(1)} %reshape.135), channel_id=1, source_target_pairs={{0,2},{2,4},{4,6},{6,0},{1,3},{3,5},{5,7},{7,1},{8,10},{10,12},{12... | collective-permute-start | bytes 3848 | tf_op jit(solution)/shard_map/ppermute | solution.py:96
  151.0 16.2 %collective-permute-start.2 = (f32[320]{0:T(512)S(1)}, f32[320]{0:T(512)S(1)}, u32[]{:S(2)}, u32[]{:S(2)}) collective-permute-start(f32[320]{0:T(512)S(1)} %reshape.135), channel_id=1, source_target_pairs={{0,4},{2,6},{4,0},{6,2},{1,5},{3,7},{5,1},{7,3},{8,12},{10,14},{12... | collective-permute-start | bytes 3848 | tf_op jit(solution)/shard_map/ppermute | solution.py:96
  153.3 13.9 %collective-permute-start.3 = (f32[320]{0:T(512)S(1)}, f32[320]{0:T(512)S(1)}, u32[]{:S(2)}, u32[]{:S(2)}) collective-permute-start(f32[320]{0:T(512)S(1)} %reshape.135), channel_id=1, source_target_pairs={{0,6},{2,0},{4,2},{6,4},{1,7},{3,1},{5,3},{7,5},{8,14},{10,8},{12,... | collective-permute-start | bytes 3848 | tf_op jit(solution)/shard_map/ppermute | solution.py:96
  170.1 378.3 %copy-start.2 = (f32[1280,640]{0,1:T(8,128)S(1)}, f32[1280,640]{0,1:T(8,128)}, u32[]{:S(2)}) copy-start(f32[1280,640]{0,1:T(8,128)} %copy.36) | copy-start | bytes 9830404
  548.4 113.8 %copy-start.13 = (f32[1280]{0:T(1024)S(1)}, f32[1280]{0:T(1024)}, u32[]{:S(2)}) copy-start(f32[1280]{0:T(1024)} %param.22) | copy-start | bytes 15364
  548.4 113.8 %copy-start.14 = (f32[1280]{0:T(1024)S(1)}, f32[1280]{0:T(1024)}, u32[]{:S(2)}) copy-start(f32[1280]{0:T(1024)} %param.21) | copy-start | bytes 15364
  554.5 112.6 %copy-start.4 = (bf16[1280,640]{0,1:T(8,128)(2,1)S(1)}, bf16[1280,640]{0,1:T(8,128)(2,1)}, u32[]{:S(2)}) copy-start(bf16[1280,640]{0,1:T(8,128)(2,1)} %copy-done.3) | copy-start | bytes 4915204
  798.7 24.9 %all-to-all-start.4 = ((bf16[4,320,640]{2,1,0:T(8,128)(2,1)}), bf16[4,320,640]{2,1,0:T(8,128)(2,1)S(1)}, u32[]{:S(2)}, u32[]{:S(2)}) async-start(bf16[4,320,640]{2,1,0:T(8,128)(2,1)} %bitcast.17), calls=%async_computation.4 | async-start | bytes 3276800 | tf_op jit(solution)/shard_map/all_to_all | solution.py:14
  823.9 26.7 %copy-start.1 = (bf16[40,3,128]{2,0,1:T(8,128)(2,1)S(1)}, bf16[40,3,128]{2,0,1:T(8,128)(2,1)}, u32[]{:S(2)}) copy-start(bf16[40,3,128]{2,0,1:T(8,128)(2,1)} %param.17) | copy-start | bytes 92164
  825.7 19.6 %collective-permute-start.5 = (bf16[160,640]{0,1:T(8,128)(2,1)S(1)}, bf16[160,640]{0,1:T(8,128)(2,1)S(1)}, u32[]{:S(2)}, u32[]{:S(2)}) collective-permute-start(bf16[160,640]{0,1:T(8,128)(2,1)S(1)} %get-tuple-element.11), channel_id=1, source_target_pairs={{0,0},{8,1},{1,8},{9,9},{2,2},{10,3},{3,10},{11,11},{4,4},{12,5},{... | collective-permute-start | bytes 614408 | tf_op jit(solution)/shard_map/ppermute | solution.py:133
  832.0 16.6 %collective-permute-start.6 = (bf16[160,640]{0,1:T(8,128)(2,1)S(1)}, bf16[160,640]{0,1:T(8,128)(2,1)S(1)}, u32[]{:S(2)}, u32[]{:S(2)}) collective-permute-start(bf16[160,640]{0,1:T(8,128)(2,1)S(1)} %get-tuple-element.12), channel_id=1, source_target_pairs={{0,1},{8,0},{1,9},{9,8},{2,3},{10,2},{3,11},{11,10},{4,5},{12,4},{... | collective-permute-start | bytes 614408 | tf_op jit(solution)/shard_map/ppermute | solution.py:134
  (7 other events, 27.7 us)
Sparse Core Ops, SparseCore 0:
  9.2 118.7 all-gather.6
  129.8 413.2 all-gather.10
  545.0 117.1 all-gather.8
  663.9 114.2 all-gather.12
where the time goes:
time: 864 us; the launch traced here: 857 us
  waiting for transfers between devices  708 us (82%)
  starting transfers between devices  35.8 us (4%)
  matrix products  32.8 us (4%)
  local copies, waits for them, and re-layouts  29.2 us (3%)
  blocking collectives  28.5 us (3%)
  between operations  13.8 us (2%)
  other arithmetic  8.8 us (1%)
    all_gather x1, waiting for transfers between devices, on_device(): w_out = lax.all_gather(out_weight, ('y',) + plane, axis=0, tiled=True)  373 us
    all_gather x1, waiting for transfers between devices, on_device(): w_two = lax.all_gather(fc2_weight, plane, axis=0, tiled=True)  108 us
    all_gather x1, waiting for transfers between devices, on_device(): w_one = lax.all_gather(fc1_weight, plane, axis=0, tiled=True)  108 us
    all_to_all x4, waiting for transfers between devices, exchange(): return lax.all_to_all(value, axes, split_axis=0, concat_axis=0, tiled=True)  52 us
    all_gather x1, waiting for transfers between devices, on_device(): lax.all_gather(qkv_weight.reshape(40, 384), plane, axis=0, tiled=True)  30.2 us
    dot_general x10, matrix products, dot_rows(): lax.dot_general(left, right, (((0,), (0,)), ((), ())), preferred_element_...  30.1 us
    all_to_all x1, blocking collectives, exchange(): return lax.all_to_all(value, axes, split_axis=0, concat_axis=0, tiled=True)  28.5 us
    all_to_all x4, starting transfers between devices, exchange(): return lax.all_to_all(value, axes, split_axis=0, concat_axis=0, tiled=True)  22.3 us
  transfers between devices with their start and end apart: 15, of which 13 were waited for; matrix products, arithmetic and copies ran while one was open for 5% of the time, Pallas kernels for 0%

commit v1 on v0

--- a/solution.py
+++ b/solution.py
@@ -8,6 +8,13 @@
 DP = ("x", "zl", "core")
 HEAD = ("y", "zh")
 EPS = 1e-05
+
+
+def exchange_gather(value, name, dim):
+    peers = lax.axis_size(name)
+    tiles = jnp.stack([value for _ in range(peers)])
+    tiles = lax.all_to_all(tiles, name, split_axis=0, concat_axis=0)
+    return jnp.concatenate(tiles, axis=dim)
 
 
 def exchange(value, axes):
@@ -81,7 +88,7 @@
     w_qkv = lax.all_gather(qkv_weight.reshape(40, 384), plane, axis=0, tiled=True)
     w_out = lax.all_gather(out_weight, ("y",) + plane, axis=0, tiled=True)
     w_one = lax.all_gather(fc1_weight, plane, axis=0, tiled=True)
-    w_two = lax.all_gather(fc2_weight, plane, axis=0, tiled=True)
+    w_two = exchange_gather(fc2_weight, plane, 0)
     own = jnp.concatenate([qv_bias[0], qv_bias[1], fc1_bias, fc2_bias, out_bias])
     other = lax.ppermute(own, "zh", [(0, 1), (1, 0)])
     both = jnp.where(zh_at == 0, jnp.stack([own, other]), jnp.stack([other, own]))

time: 864 us -> 780 us (0.903)
  waiting for transfers between devices: 708 us -> 613 us
    all_gather x1 -> x0, waiting for transfers between devices: 108 us -> none  [on_device(): w_two = lax.all_gather(fc2_weight, plane, axis=0, tiled=True)]
    all_gather x1, waiting for transfers between devices: 30.2 us -> 48.2 us  [on_device(): lax.all_gather(qkv_weight.reshape(40, 384), plane, axis=0, tiled=True)]
    all_to_all x4, waiting for transfers between devices: 52 us -> 64.9 us  [exchange(): return lax.all_to_all(value, axes, split_axis=0, concat_axis=0, tiled=True)]
    ppermute x3, waiting for transfers between devices: 12.5 us -> 1.83 us  [on_device(): lax.ppermute(out_pair, 'y', [(at, (at + step) % 4) for at in range(4)])]
    all_to_all x0 -> x1, starting transfers between devices: none -> 9.47 us  [exchange_gather(): tiles = lax.all_to_all(tiles, name, split_axis=0, concat_axis=0)]
  transfers between devices with their start and end apart: 15 -> 15, of which waited for: 13 -> 14; matrix products, arithmetic and copies ran while one was open for 5% -> 5% of each run, Pallas kernels for 0% -> 0%
where the time goes in v1:
time: 780 us; the launch traced here: 770 us
  waiting for transfers between devices  613 us (79%)
  starting transfers between devices  44.1 us (6%)
  matrix products  32.8 us (4%)
  local copies, waits for them, and re-layouts  29.4 us (4%)
  blocking collectives  26.5 us (3%)
  between operations  15.5 us (2%)
  other arithmetic  8.81 us (1%)
    all_gather x1, waiting for transfers between devices, on_device(): w_out = lax.all_gather(out_weight, ('y',) + plane, axis=0, tiled=True)  374 us
    all_gather x1, waiting for transfers between devices, on_device(): w_one = lax.all_gather(fc1_weight, plane, axis=0, tiled=True)  105 us
    all_to_all x4, waiting for transfers between devices, exchange(): return lax.all_to_all(value, axes, split_axis=0, concat_axis=0, tiled=True)  64.9 us
    all_gather x1, waiting for transfers between devices, on_device(): lax.all_gather(qkv_weight.reshape(40, 384), plane, axis=0, tiled=True)  48.2 us
    dot_general x10, matrix products, dot_rows(): lax.dot_general(left, right, (((0,), (0,)), ((), ())), preferred_element_...  30 us
    all_to_all x1, blocking collectives, exchange(): return lax.all_to_all(value, axes, split_axis=0, concat_axis=0, tiled=True)  26.5 us
    all_to_all x4, starting transfers between devices, exchange(): return lax.all_to_all(value, axes, split_axis=0, concat_axis=0, tiled=True)  21.9 us
  transfers between devices with their start and end apart: 15, of which 14 were waited for; matrix products, arithmetic and copies ran while one was open for 5% of the time, Pallas kernels for 0%

profile of v1, /device:TPU:3, one launch (start us, length us, event | category | flops | bytes accessed | tf_op | source)
XLA Modules:
  0.0 770.4 jit_solution(454032891740214003)
XLA Ops:
  11.0 9.3 %all-to-all-start = ((bf16[32,10,640]{2,1,0:T(8,128)(2,1)}), bf16[32,10,640]{2,1,0:T(8,128)(2,1)S(1)}, u32[]{:S(2)}, u32[]{:S(2)}) async-start(bf16[32,10,640]{2,1,0:T(8,128)(2,1)} %reshape.138), calls=%async_computation | async-start | bytes 1310720 | tf_op jit(solution)/shard_map/all_to_all | solution.py:21
  21.8 15.7 %all-to-all-done = bf16[32,10,640]{2,1,0:T(8,128)(2,1)S(1)} async-done(((bf16[32,10,640]{2,1,0:T(8,128)(2,1)}), bf16[32,10,640]{2,1,0:T(8,128)(2,1)S(1)}, u32[]{:S(2)}, u32[]{:S(2)}) %all-to-all-start) | async-done | bytes 409632 | tf_op jit(solution)/shard_map/all_to_all | solution.py:21
  38.4 26.5 %all_to_all.30 = bf16[32,10,640]{2,1,0:T(8,128)(2,1)S(1)} all-to-all(bf16[32,10,640]{2,1,0:T(8,128)(2,1)S(1)} %broadcast_select_fusion), channel_id=1, replica_groups=mesh['x'=4,'zl'=4,'core'=2,'y'=4,'zh'=2] {'zh','x','zl'}, dimensions={0} | all-to-all | bytes 819200 | tf_op jit(solution)/shard_map/all_to_all | solution.py:21
  66.4 4.6 all-to-all-start.2
  73.4 4.1 collective-permute-done
  77.5 11.5 %all-to-all-done.2 = bf16[4,320,640]{2,1,0:T(8,128)(2,1)S(1)} async-done(((bf16[4,320,640]{2,1,0:T(8,128)(2,1)}), bf16[4,320,640]{2,1,0:T(8,128)(2,1)S(1)}, u32[]{:S(2)}, u32[]{:S(2)}) %all-to-all-start.2) | async-done | bytes 1638432 | tf_op jit(solution)/shard_map/all_to_all | solution.py:21
  90.5 48.2 %all-gather.5.cloned.1.call-done = bf16[2560,384]{1,0:T(8,128)(2,1)} async-done(((bf16[40,384]{1,0:T(8,128)(2,1)}), bf16[2560,384]{1,0:T(8,128)(2,1)}) %all-gather.5.cloned.1.call-update) | async-done | bytes 1966096 | tf_op jit(solution)/shard_map/all_gather | solution.py:88
  155.8 4.0 all-to-all-start.3
  160.4 16.9 %all-to-all-done.3 = bf16[4,256,640]{2,1,0:T(8,128)(2,1)S(1)} async-done(((bf16[4,256,640]{2,1,0:T(8,128)(2,1)}), bf16[4,256,640]{2,1,0:T(8,128)(2,1)S(1)}, u32[]{:S(2)}, u32[]{:S(2)}) %all-to-all-start.3) | async-done | bytes 1310752 | tf_op jit(solution)/shard_map/all_to_all | solution.py:21
  179.4 9.5 %all-to-all-start.4 = ((bf16[64,20,1280]{2,1,0:T(8,128)(2,1)}), bf16[64,20,1280]{2,1,0:T(8,128)(2,1)}, u32[]{:S(2)}, u32[]{:S(2)}) async-start(bf16[64,20,1280]{2,1,0:T(8,128)(2,1)} %stack.22), calls=%async_computation.4 | async-start | bytes 7864320 | tf_op jit(solution)/shard_map/all_to_all | solution.py:16
  194.2 2.5 copy.36
  196.7 374.4 %all-gather.9.cloned.1.call-done = bf16[256,4,1280]{2,1,0:T(4,128)(2,1)} async-done(((bf16[1,4,1280]{2,1,0:T(4,128)(2,1)}), bf16[256,4,1280]{2,1,0:T(4,128)(2,1)}) %all-gather.9.cloned.1.call-update) | async-done | bytes 2621456 | tf_op jit(solution)/shard_map/all_gather | solution.py:89
  571.1 5.3 reshape.156
  576.4 4.8 convert_reduce_fusion
  581.9 104.6 %all-gather.7.cloned.1.call-done = bf16[2560,640]{1,0:T(8,128)(2,1)} async-done(((bf16[40,640]{1,0:T(8,128)(2,1)}), bf16[2560,640]{1,0:T(8,128)(2,1)}) %all-gather.7.cloned.1.call-update) | async-done | bytes 3276816 | tf_op jit(solution)/shard_map/all_gather | solution.py:90
  686.4 4.5 fusion.61
  690.9 3.0 fusion.64
  693.9 6.3 reshape.143
  700.3 11.9 %fusion.20 = bf16[1280,640]{0,1:T(8,128)(2,1)S(1)} fusion(bf16[1280,1280]{1,0:T(8,128)(2,1)} %reshape.143, f32[640,640]{1,0:T(8,128)} %fusion.64, f32[640,640]{1,0:T(8,128)} %fusion.61, f32[1280]{0:T(1024)S(1)} %add.183), kind=kOutput, calls=%fused_computation.47 | convolution fusion | flops 2152857600 | bytes 8197120 | tf_op jit(solution)/shard_map/dot_general | solution.py:39
  714.4 4.0 all-to-all-start.5
  718.5 20.9 %all-to-all-done.5 = bf16[4,320,640]{2,1,0:T(8,128)(2,1)S(1)} async-done(((bf16[4,320,640]{2,1,0:T(8,128)(2,1)}), bf16[4,320,640]{2,1,0:T(8,128)(2,1)S(1)}, u32[]{:S(2)}, u32[]{:S(2)}) %all-to-all-start.5) | async-done | bytes 1638432 | tf_op jit(solution)/shard_map/all_to_all | solution.py:21
  741.4 6.6 collective-permute-start.5
  748.1 8.3 %collective-permute-done.5 = bf16[160,640]{0,1:T(8,128)(2,1)S(1)} collective-permute-done((bf16[160,640]{0,1:T(8,128)(2,1)S(1)}, bf16[160,640]{0,1:T(8,128)(2,1)S(1)}, u32[]{:S(2)}, u32[]{:S(2)}) %collective-permute-start.5) | collective-permute-done | bytes 204832 | tf_op jit(solution)/shard_map/ppermute | solution.py:140
  756.5 4.4 collective-permute-done.6
  (126 shorter events, 43.1 us)
Async XLA Ops:
  7.4 13.1 %copy-start = (bf16[40,3,128]{2,0,1:T(8,128)(2,1)S(1)}, bf16[40,3,128]{2,0,1:T(8,128)(2,1)}, u32[]{:S(2)}) copy-start(bf16[40,3,128]{2,0,1:T(8,128)(2,1)} %param.17) | copy-start | bytes 92164
  7.4 13.8 %copy-start.14 = (s32[32]{0:T(128)S(1)}, s32[32]{0:T(128)}, u32[]{:S(2)}) copy-start(s32[32]{0:T(128)} %param.27) | copy-start | bytes 388
  11.0 26.5 %all-to-all-start = ((bf16[32,10,640]{2,1,0:T(8,128)(2,1)}), bf16[32,10,640]{2,1,0:T(8,128)(2,1)S(1)}, u32[]{:S(2)}, u32[]{:S(2)}) async-start(bf16[32,10,640]{2,1,0:T(8,128)(2,1)} %reshape.138), calls=%async_computation | async-start | bytes 1310720 | tf_op jit(solution)/shard_map/all_to_all | solution.py:21
  20.4 118.2 %all-gather.5.cloned.1.call-start = ((), (), s32[]{:S(2)}) async-start(), calls=%async_computation.6 | async-start | bytes 1996800 | tf_op jit(solution)/shard_map/all_gather | solution.py:88
  66.4 23.5 %copy-start.4 = (f32[1280]{0:T(1024)S(1)}, f32[1280]{0:T(1024)}, u32[]{:S(2)}) copy-start(f32[1280]{0:T(1024)} %param.16) | copy-start | bytes 15364
  66.4 23.5 %copy-start.5 = (f32[1280]{0:T(1024)S(1)}, f32[1280]{0:T(1024)}, u32[]{:S(2)}) copy-start(f32[1280]{0:T(1024)} %param.15) | copy-start | bytes 15364
  66.4 22.6 %all-to-all-start.2 = ((bf16[4,320,640]{2,1,0:T(8,128)(2,1)}), bf16[4,320,640]{2,1,0:T(8,128)(2,1)S(1)}, u32[]{:S(2)}, u32[]{:S(2)}) async-start(bf16[4,320,640]{2,1,0:T(8,128)(2,1)} %broadcast_in_dim.38), calls=%async_computation.2 | async-start | bytes 3276800 | tf_op jit(solution)/shard_map/all_to_all | solution.py:21
  70.9 500.2 %all-gather.9.cloned.1.call-start = ((), (), s32[]{:S(2)}) async-start(), calls=%async_computation.8 | async-start | bytes 2631680 | tf_op jit(solution)/shard_map/all_gather | solution.py:89
  71.0 6.4 collective-permute-start
  143.1 2.9 collective-permute-start.4
  154.6 22.7 %copy-start.3 = (bf16[20,1280]{1,0:T(8,128)(2,1)S(1)}, bf16[20,1280]{1,0:T(8,128)(2,1)}, u32[]{:S(2)}) copy-start(bf16[20,1280]{1,0:T(8,128)(2,1)} %param.25) | copy-start | bytes 153604
  155.8 21.5 %all-to-all-start.3 = ((bf16[4,256,640]{2,1,0:T(8,128)(2,1)}), bf16[4,256,640]{2,1,0:T(8,128)(2,1)S(1)}, u32[]{:S(2)}, u32[]{:S(2)}) async-start(bf16[4,256,640]{2,1,0:T(8,128)(2,1)} %broadcast_in_dim.43), calls=%async_computation.3 | async-start | bytes 2621440 | tf_op jit(solution)/shard_map/all_to_all | solution.py:21
  159.8 526.6 %all-gather.7.cloned.1.call-start = ((), (), s32[]{:S(2)}) async-start(), calls=%async_computation.7 | async-start | bytes 3328000 | tf_op jit(solution)/shard_map/all_gather | solution.py:90
  179.4 514.5 %all-to-all-start.4 = ((bf16[64,20,1280]{2,1,0:T(8,128)(2,1)}), bf16[64,20,1280]{2,1,0:T(8,128)(2,1)}, u32[]{:S(2)}, u32[]{:S(2)}) async-start(bf16[64,20,1280]{2,1,0:T(8,128)(2,1)} %stack.22), calls=%async_computation.4 | async-start | bytes 7864320 | tf_op jit(solution)/shard_map/all_to_all | solution.py:16
  189.1 3.9 collective-permute-start.1
  189.4 4.3 collective-permute-start.2
  191.1 2.8 collective-permute-start.3
  576.4 110.0 %copy-start.12 = (f32[1280]{0:T(1024)S(1)}, f32[1280]{0:T(1024)}, u32[]{:S(2)}) copy-start(f32[1280]{0:T(1024)} %param.22) | copy-start | bytes 15364
  576.4 110.0 %copy-start.13 = (f32[1280]{0:T(1024)S(1)}, f32[1280]{0:T(1024)}, u32[]{:S(2)}) copy-start(f32[1280]{0:T(1024)} %param.21) | copy-start | bytes 15364
  581.3 109.7 %copy-start.2 = (bf16[1280,640]{0,1:T(8,128)(2,1)}, bf16[1280,640]{0,1:T(8,128)(2,1)S(1)}, u32[]{:S(2)}) copy-start(bf16[1280,640]{0,1:T(8,128)(2,1)S(1)} %get-tuple-element.6) | copy-start | bytes 4915204
  714.4 24.9 %all-to-all-start.5 = ((bf16[4,320,640]{2,1,0:T(8,128)(2,1)}), bf16[4,320,640]{2,1,0:T(8,128)(2,1)S(1)}, u32[]{:S(2)}, u32[]{:S(2)}) async-start(bf16[4,320,640]{2,1,0:T(8,128)(2,1)} %bitcast.16), calls=%async_computation.5 | async-start | bytes 3276800 | tf_op jit(solution)/shard_map/all_to_all | solution.py:21
  739.5 23.2 %copy-start.1 = (bf16[40,3,128]{2,0,1:T(8,128)(2,1)S(1)}, bf16[40,3,128]{2,0,1:T(8,128)(2,1)}, u32[]{:S(2)}) copy-start(bf16[40,3,128]{2,0,1:T(8,128)(2,1)} %param.17) | copy-start | bytes 92164
  741.4 15.1 %collective-permute-start.5 = (bf16[160,640]{0,1:T(8,128)(2,1)S(1)}, bf16[160,640]{0,1:T(8,128)(2,1)S(1)}, u32[]{:S(2)}, u32[]{:S(2)}) collective-permute-start(bf16[160,640]{0,1:T(8,128)(2,1)S(1)} %get-tuple-element.11), channel_id=1, source_target_pairs={{0,0},{8,1},{1,8},{9,9},{2,2},{10,3},{3,10},{11,11},{4,4},{12,5},{... | collective-permute-start | bytes 614408 | tf_op jit(solution)/shard_map/ppermute | solution.py:140
  748.0 12.9 %collective-permute-start.6 = (bf16[160,640]{0,1:T(8,128)(2,1)S(1)}, bf16[160,640]{0,1:T(8,128)(2,1)S(1)}, u32[]{:S(2)}, u32[]{:S(2)}) collective-permute-start(bf16[160,640]{0,1:T(8,128)(2,1)S(1)} %get-tuple-element.12), channel_id=1, source_target_pairs={{0,1},{8,0},{1,9},{9,8},{2,3},{10,2},{3,11},{11,10},{4,5},{12,4},{... | collective-permute-start | bytes 614408 | tf_op jit(solution)/shard_map/ppermute | solution.py:141
  (6 other events, 31.0 us)
Sparse Core Ops, SparseCore 0:
  23.1 115.5 all-gather.4
Sparse Core Ops, SparseCore 1:
  144.0 427.1 all-gather.8
  572.9 113.5 all-gather.6
